TPU v7x, 256 devices: a whole 4x4x8 slice. The times are simulated.
256 devices in a mesh: ep: 64 (over z, y, core), fsdp: 4 (over x).
Axes of the slice: x: 4, y: 4, z: 8, core: 2. Of those that a mesh axis runs over, the one named last changes fastest.
Arguments:
- train_gate: float32 [64, 2048, 1024], P('ep', 'fsdp'), may hold values from -0.1875 to 0.1875
- other_gate: float32 [64, 2048, 1024], P('ep', 'fsdp'), may hold values from -0.125 to 0.125
- train_up: float32 [64, 2048, 1024], P('ep', 'fsdp'), may hold values from -0.1875 to 0.1875
- other_up: float32 [64, 2048, 1024], P('ep', 'fsdp'), may hold values from -0.125 to 0.125
- mix_share: float32 [64], P('ep'), may hold values from 0.2 to 0.8
- router_weight: float32 [2048, 64], P('fsdp', 'ep'), may hold values from -0.125 to 0.125
- router_gain: float32 [2048], P('fsdp'), may hold values from 0.25 to 1.75
Outputs:
- ready_gate: bfloat16 [64, 2048, 1024], P('ep')
- ready_up: bfloat16 [64, 2048, 1024], P('ep')
- scale_gate: float32 [64, 1024], P('ep')
- scale_up: float32 [64, 1024], P('ep')
- serve_router: bfloat16 [2048, 64], replicated
All inputs are finite; a program needn't handle non-finite values. Where the computation divides by a largest or mean magnitude, that divisor is 1e-20 or more.
Results may differ from a plain program's by a relative error of at most 0.001.
Values may be sent and summed in bfloat16 or wider, within the bound.
A program may use at most 64 MiB of HBM per device.

v0:
```python
import jax
import jax.numpy as jnp
from jax import lax
from jax.sharding import PartitionSpec as P


def sent_to_all(array, axis):
    length = lax.axis_size(axis)
    return lax.all_to_all(
        jnp.broadcast_to(array[None], (length, *array.shape)), axis, 0, 0, tiled=True
    )


def of_everyone(array, axis):
    everything = sent_to_all(array, axis)
    return jnp.max(everything, axis=0)


def together(arrays, axis):
    ends = [0]
    for a in arrays:
        ends.append(ends[-1] + a.size)
    subtotal = of_everyone(jnp.concatenate([a.ravel() for a in arrays]), axis)
    return tuple((subtotal[b:e].reshape(a.shape) for a, b, e in zip(arrays, ends, ends[1:])))


def side_by_side(arrays, axis, dim, along):
    widths = [a.shape[along] for a in arrays]
    both = jnp.concatenate(arrays, axis=along)
    out = lax.all_gather(both, axis, axis=dim, tiled=True)
    return tuple(jnp.split(out, [sum(widths[:k]) for k in range(1, len(widths))], axis=along))


def joined_along(pieces, dim):
    pieces = jnp.moveaxis(pieces, 0, dim)
    dims = pieces.shape
    return pieces.reshape(*dims[:dim], dims[dim] * dims[dim + 1], *dims[dim + 2 :])


def gathered_copies(array, axis, dim):
    pieces = sent_to_all(array, axis)
    return joined_along(pieces, dim)


def per_device(train_gate, other_gate, train_up, other_up, mix_share, router_weight, router_gain):
    latest_gate = (
        mix_share[:, None, None] * train_gate + (1.0 - mix_share[:, None, None]) * other_gate
    )
    latest_up = mix_share[:, None, None] * train_up + (1.0 - mix_share[:, None, None]) * other_up
    scale_gate, scale_up = together(
        (jnp.max(jnp.abs(latest_gate), axis=1), jnp.max(jnp.abs(latest_up), axis=1)), "fsdp"
    )
    narrow_gate, narrow_up = (
        (latest_gate / jnp.expand_dims(scale_gate, 1)).astype(jnp.bfloat16),
        (latest_up / jnp.expand_dims(scale_up, 1)).astype(jnp.bfloat16),
    )
    ready_gate, ready_up = side_by_side((narrow_gate, narrow_up), "fsdp", 1, 0)
    part_router = (router_weight * router_gain[:, None]).astype(jnp.bfloat16)
    row_router = lax.all_gather(part_router, "fsdp", axis=0, tiled=True)
    serve_router = gathered_copies(row_router, "ep", 1)
    return (ready_gate, ready_up, scale_gate, scale_up, serve_router)


def solution(mesh):
    placed = (
        P("ep", "fsdp", None),
        P("ep", "fsdp", None),
        P("ep", "fsdp", None),
        P("ep", "fsdp", None),
        P("ep"),
        P("fsdp", "ep"),
        P("fsdp"),
    )
    return jax.shard_map(
        per_device,
        mesh=mesh,
        in_specs=placed,
        out_specs=(P("ep", None, None), P("ep", None, None), P("ep", None), P("ep", None), P()),
        check_vma=False,
    )
```

profile of v0, /device:TPU:1, one launch (start us, length us, event | category | flops | bytes accessed | tf_op | source)
XLA Modules:
  0.0 127.2 jit_solution(10108246183193982940)
XLA Ops:
  7.2 0.0 all-gather.2.cloned.1.call-start
  7.9 0.0 copy-start
  7.9 0.0 copy-start.1
  7.9 2.6 %abs_reduce_fusion.1 = f32[1024]{0:T(1024)S(1)} fusion(f32[1,512,1024]{2,1,0:T(8,128)} %param.8, f32[]{:T(128)} %bitcast.1, f32[1,512,1024]{2,1,0:T(8,128)} %param.7, f32[]{:T(128)} %bitcast.13), kind=kLoop, calls=%fused_computation.5 | loop fusion | flops 2620416 | bytes 4198408 | tf_op jit(solution)/shard_map/reduce_max | solution.py:51
  10.5 0.2 copy-done
  10.7 0.6 copy-done.1
  11.3 0.3 abs_reduce_fusion
  11.7 8.9 %all_to_all.11 = f32[4,1,2048]{2,1,0:T(1,128)S(1)} all-to-all(f32[4,1,2048]{2,1,0:T(1,128)S(1)} %broadcast_in_dim.8), channel_id=1, replica_groups=mesh['ep'=64,'fsdp'=4] {'fsdp'}, dimensions={0} | all-to-all | bytes 65536 | tf_op jit(solution)/shard_map/all_to_all | solution.py:9
  20.7 0.0 copy-start.2
  20.7 0.0 copy-start.3
  20.7 4.0 %divide_convert_fusion = (bf16[1,512,1024]{2,1,0:T(8,128)(2,1)S(1)}, bf16[1,512,1024]{2,1,0:T(8,128)(2,1)S(1)}) fusion(f32[1024]{0:T(1024)S(1)} %get-tuple-element.8, f32[1,512,1024]{2,1,0:T(8,128)S(1)} %copy-done, f32[]{:T(128)} %bitcast.1, f32[1,512,1024]{2,1,0:T(8,128)} %param.9, f32[]{:T(128)} %bitcast.15, f32[1024]{0:T(1024)S(1)} %get-tuple-element.7, ...), kind=kLoop, calls=%fused_computation.1 | loop fusion | flops 5242880 | bytes 10493960 | tf_op jit(solution)/shard_map/convert_element_type | solution.py:55
  24.6 0.0 copy-done.2
  24.7 0.0 copy-done.3
  24.7 1.5 %pad_maximum_fusion = bf16[2,512,1024]{2,1,0:T(8,128)(2,1)} fusion(bf16[1,512,1024]{2,1,0:T(8,128)(2,1)S(1)} %get-tuple-element.9, bf16[1,512,1024]{2,1,0:T(8,128)(2,1)S(1)} %get-tuple-element.10), kind=kLoop, calls=%fused_computation | loop fusion | flops 1048576 | bytes 4194304 | tf_op jit(solution)/shard_map/concatenate | solution.py:29
  26.2 0.0 copy-start.4
  26.2 0.0 copy-start.5
  26.2 0.0 all-gather.2.cloned.1.call-update
  26.2 0.7 copy-done.4
  26.9 0.0 copy-done.5
  26.9 8.1 %all_gather.7 = bf16[2048,1]{0,1:T(2,128)(2,1)S(1)} all-gather(bf16[512,1]{0,1:T(2,128)(2,1)S(1)} %multiply_convert_fusion), channel_id=1, replica_groups=mesh['ep'=64,'fsdp'=4] {'fsdp'}, dimensions={0}, use_global_device_ids=true | all-gather | bytes 5120 | tf_op jit(solution)/shard_map/all_gather | solution.py:59
  35.0 0.3 broadcast_bitcast_fusion
  35.3 0.5 broadcast.11
  35.8 2.2 %reduce.4 = bf16[64,2048]{1,0:T(8,128)(2,1)S(1)} reduce(bf16[64,1,2048]{2,1,0:T(2,128)(2,1)S(1)} %broadcast_bitcast_fusion, bf16[]{:T(256)} %broadcast.11), dimensions={1}, to_apply=%broadcast_bitcast_fusion.reduce_sub_computation | reduce | bytes 524290
  38.0 0.2 reshape.52
  38.2 28.9 %all_to_all.12 = bf16[64,2,1024]{2,1,0:T(2,128)(2,1)S(1)} all-to-all(bf16[64,2,1024]{2,1,0:T(2,128)(2,1)S(1)} %reshape.52), channel_id=1, replica_groups=mesh['ep'=64,'fsdp'=4] {'ep'}, dimensions={0} | all-to-all | bytes 524288 | tf_op jit(solution)/shard_map/all_to_all | solution.py:9
  67.1 0.2 reshape.53
  67.3 0.9 copy.20
  68.2 46.1 %all-gather.2.cloned.1.call-done = bf16[2,2048,1024]{2,1,0:T(8,128)(2,1)} async-done(((bf16[2,512,1024]{2,1,0:T(8,128)(2,1)}), bf16[2,2048,1024]{2,1,0:T(8,128)(2,1)}) %all-gather.2.cloned.1.call-update) | async-done | bytes 8388624 | tf_op jit(solution)/shard_map/all_gather | solution.py:30
  114.3 6.0 %fusion = (bf16[1,2048,1024]{2,1,0:T(8,128)(2,1)}, bf16[1,2048,1024]{2,1,0:T(8,128)(2,1)}) fusion(bf16[2,2048,1024]{2,1,0:T(8,128)(2,1)} %all-gather.2.cloned.1.call-done), kind=kLoop, calls=%fused_computation.10 | loop fusion | bytes 16777216 | tf_op jit(solution)/shard_map/split | solution.py:31
  (6 shorter events, 0.1 us)
Async XLA Ops:
  7.2 107.2 %all-gather.2.cloned.1.call-start = ((), (), s32[]{:S(2)}) async-start(), calls=%async_computation.2 | async-start | bytes 10485760 | tf_op jit(solution)/shard_map/all_gather | solution.py:30
  7.9 2.9 %copy-start = (f32[1,512,1024]{2,1,0:T(8,128)S(1)}, f32[1,512,1024]{2,1,0:T(8,128)}, u32[]{:S(2)}) copy-start(f32[1,512,1024]{2,1,0:T(8,128)} %param.10) | copy-start | bytes 6291460
  7.9 3.5 %copy-start.1 = (f32[1,512,1024]{2,1,0:T(8,128)S(1)}, f32[1,512,1024]{2,1,0:T(8,128)}, u32[]{:S(2)}) copy-start(f32[1,512,1024]{2,1,0:T(8,128)} %param.9) | copy-start | bytes 6291460
  20.7 4.0 %copy-start.2 = (f32[1024]{0:T(1024)}, f32[1024]{0:T(1024)S(1)}, u32[]{:S(2)}) copy-start(f32[1024]{0:T(1024)S(1)} %get-tuple-element.7) | copy-start | bytes 12292
  20.7 4.0 %copy-start.3 = (f32[1024]{0:T(1024)}, f32[1024]{0:T(1024)S(1)}, u32[]{:S(2)}) copy-start(f32[1024]{0:T(1024)S(1)} %get-tuple-element.8) | copy-start | bytes 12292
  26.2 0.7 copy-start.4
  26.2 0.7 copy-start.5
Sparse Core Ops, SparseCore 0:
  26.3 87.9 all-gather.1
where the time goes:
time: 127 us
  waiting for transfers between devices  46.1 us (36%)
  blocking collectives  46 us (36%)
  between operations  14.8 us (12%)
  other arithmetic  10.6 us (8%)
  local copies, waits for them, and re-layouts  9.61 us (8%)
    all_gather x1, waiting for transfers between devices, side_by_side(): out = lax.all_gather(both, axis, axis=dim, tiled=True)  46.1 us
    all_to_all x2, blocking collectives, sent_to_all(): lax.all_to_all(jnp.broadcast_to(array[None], (length, *array.shape)), axi...  37.9 us
    all_gather x1, blocking collectives, per_device(): row_router = lax.all_gather(part_router, 'fsdp', axis=0, tiled=True)  8.13 us
    split x1, local copies, waits for them, and re-layouts, side_by_side(): jnp.split(out, [sum(widths[:k]) for k in range(1, len(widths))], axis=along)  6.02 us
    convert_element_type x1, other arithmetic, per_device(): (latest_up / jnp.expand_dims(scale_up, 1)).astype(jnp.bfloat16)  3.95 us
    unnamed x16, local copies, waits for them, and re-layouts  2.71 us
    reduce_max x1, other arithmetic, per_device(): jnp.max(jnp.abs(latest_gate), axis=1)  2.63 us
  transfers between devices with their start and end apart: 1, of which 1 were waited for; matrix products, arithmetic and copies ran while one was open for 3% of the time, Pallas kernels for 0%

commit v1 on v0

v1 whole, which is shorter than its diff:
```python
import functools

import jax
import jax.numpy as jnp
from jax import lax
from jax.experimental import pallas as pl
from jax.experimental.pallas import tpu as pltpu
from jax.sharding import PartitionSpec as P

MESH = pl.DeviceIdType.MESH
X, Y, Z = 4, 4, 8
ROWS, COLS = 512, 1024
WIDTH = 256
PER = COLS // WIDTH
CHUNKS = 2 * PER
HALF = ROWS // 2
STEP = 64


def main_kernel(
    share, tg, og, tu, ou, rw, rg,
    out, sc, rout,
    tbuf, obuf, mx, rwv, rgv, rt, stage,
    ld_sem, small_sem, mx_send, mx_recv, own_send, own_recv, fwd_send, fwd_recv,
    r1_send, r1_recv, r2_send, r2_recv, r3_send, r3_recv, r4_send, r4_recv,
):
    x = lax.axis_index("fsdp")
    ep = lax.axis_index("ep")
    core = lax.rem(ep, 2)
    y = lax.rem(ep // 2, Y)
    z = ep // (2 * Y)

    right, left, opp = (lax.rem(x + k, X) for k in (1, X - 1, 2))
    x_peers = tuple({"fsdp": p} for p in (right, left, opp))
    at = lambda zz, yy, cc: {"ep": (zz * Y + yy) * 2 + cc}
    y_peers = tuple(at(z, lax.rem(y + k, Y), core) for k in (1, 2, 3))
    z_up, z_down = lax.rem(z + 1, Z), lax.rem(z + Z - 1, Z)
    z_peers = (at(z_up, y, core), at(z_down, y, core))
    partner = at(z, y, 1 - core)

    barrier = pltpu.get_barrier_semaphore()
    for peer in (*x_peers, *y_peers, *z_peers, partner):
        pl.semaphore_signal(barrier, inc=1, device_id=peer, device_id_type=MESH)

    def load(j, which):
        src = ((tg, og), (tu, ou))[j // PER][which]
        cols = pl.ds((j % PER) * WIDTH, WIDTH)
        return pltpu.make_async_copy(
            src.at[0, :, cols], (tbuf, obuf)[which].at[j], ld_sem.at[j, which]
        )

    small = (
        pltpu.make_async_copy(rw, rwv, small_sem.at[0]),
        pltpu.make_async_copy(rg, rgv, small_sem.at[1]),
    )
    for j in range(CHUNKS):
        load(j, 0).start()
        load(j, 1).start()
    for c in small:
        c.start()

    def max_copy(j, k):
        return pltpu.make_async_remote_copy(
            src_ref=mx.at[j, x], dst_ref=mx.at[j, x],
            send_sem=mx_send.at[j, k], recv_sem=mx_recv.at[j, k],
            device_id=x_peers[k], device_id_type=MESH,
        )

    def own_copy(j, d, h):
        piece = out.at[j, x, pl.ds(h * HALF, HALF)]
        return pltpu.make_async_remote_copy(
            src_ref=piece, dst_ref=piece,
            send_sem=own_send.at[j, d, h], recv_sem=own_recv.at[j, d, h],
            device_id=x_peers[d], device_id_type=MESH,
        )

    def forward_copy(j, d):
        source = (left, right)[d]
        piece = out.at[j, source, pl.ds(d * HALF, HALF)]
        return pltpu.make_async_remote_copy(
            src_ref=piece, dst_ref=piece,
            send_sem=fwd_send.at[j, d], recv_sem=fwd_recv.at[j, d],
            device_id=x_peers[d], device_id_type=MESH,
        )

    share_t = share[0]
    share_o = 1.0 - share_t

    for j in range(CHUNKS):
        load(j, 0).wait()
        load(j, 1).wait()

        def mix(i, top):
            rows = pl.ds(pl.multiple_of(i * STEP, STEP), STEP)
            latest = share_t * tbuf[j, rows, :] + share_o * obuf[j, rows, :]
            tbuf[j, rows, :] = latest
            return jnp.maximum(top, jnp.max(jnp.abs(latest).reshape(STEP // 8, 8, WIDTH), axis=0))

        top = lax.fori_loop(0, ROWS // STEP, mix, jnp.zeros((8, WIDTH), jnp.float32), unroll=True)
        mx[j, x] = jnp.max(top, axis=0, keepdims=True)
        if j == 0:
            pl.semaphore_wait(barrier, 9)
        for k in (2, 0, 1):
            max_copy(j, k).start()

    for j in range(CHUNKS):
        for k in range(3):
            max_copy(j, k).wait_recv()
        scale = jnp.maximum(
            jnp.maximum(mx[j, 0], mx[j, 1]), jnp.maximum(mx[j, 2], mx[j, 3])
        )
        sc[j] = scale

        def divide(i, carry):
            rows = pl.ds(pl.multiple_of(i * STEP, STEP), STEP)
            out[j, x, rows, :] = (tbuf[j, rows, :] / scale).astype(jnp.bfloat16)
            return carry

        lax.fori_loop(0, ROWS // STEP, divide, 0, unroll=True)
        for h in range(2):
            own_copy(j, 0, h).start()
            own_copy(j, 1, 1 - h).start()

    for c in small:
        c.wait()
    piece = rwv[...] * rgv[...]
    for r in range(4):
        rt[core, z, y, x, pl.ds(r, 1), :] = piece[:, r * 128 : (r + 1) * 128]

    def r1(k):
        ref = rt.at[core, z, y, x]
        return pltpu.make_async_remote_copy(
            src_ref=ref, dst_ref=ref, send_sem=r1_send.at[k], recv_sem=r1_recv.at[k],
            device_id=x_peers[k], device_id_type=MESH,
        )

    def r2(k):
        ref = rt.at[core, z, y]
        return pltpu.make_async_remote_copy(
            src_ref=ref, dst_ref=ref, send_sem=r2_send.at[k], recv_sem=r2_recv.at[k],
            device_id=y_peers[k], device_id_type=MESH,
        )

    def r3(k, d):
        source = lax.rem(z + (Z - k if d == 0 else k), Z)
        ref = rt.at[core, source]
        return pltpu.make_async_remote_copy(
            src_ref=ref, dst_ref=ref, send_sem=r3_send.at[k, d], recv_sem=r3_recv.at[k, d],
            device_id=z_peers[d], device_id_type=MESH,
        )

    r4 = pltpu.make_async_remote_copy(
        src_ref=rt.at[core], dst_ref=rt.at[core], send_sem=r4_send, recv_sem=r4_recv,
        device_id=partner, device_id_type=MESH,
    )
    for k in range(3):
        r1(k).start()
    for k in range(3):
        r1(k).wait_recv()
    for k in range(3):
        r2(k).start()
    for k in range(3):
        r2(k).wait_recv()
    for k in range(Z // 2):
        r3(k, 0).start()
        if k < Z // 2 - 1:
            r3(k, 1).start()
        r3(k, 0).wait_recv()
        if k < Z // 2 - 1:
            r3(k, 1).wait_recv()
    r4.start()
    r4.wait_recv()

    def spread(zz, carry):
        rows = pl.ds(pl.multiple_of(zz * 2 * Y, 2 * Y), 2 * Y)
        for xx in range(X):
            for r in range(4):
                stage[rows, (xx * 4 + r) * 128 : (xx * 4 + r + 1) * 128] = jnp.concatenate(
                    [rt[e % 2, zz, e // 2, xx, pl.ds(r, 1), :] for e in range(2 * Y)], axis=0
                )
        return carry

    lax.fori_loop(0, Z, spread, 0)

    def narrow(i, carry):
        rows = pl.ds(pl.multiple_of(i * 16, 16), 16)
        rout[rows, :] = stage[rows, :].astype(jnp.bfloat16)
        return carry

    lax.fori_loop(0, 4, narrow, 0)

    for j in range(CHUNKS):
        own_copy(j, 0, 0).wait_recv()
        forward_copy(j, 0).start()
        own_copy(j, 1, 1).wait_recv()
        forward_copy(j, 1).start()

    for j in range(CHUNKS):
        own_copy(j, 0, 1).wait_recv()
        own_copy(j, 1, 0).wait_recv()
        for d in range(2):
            for h in range(2):
                own_copy(j, d, h).wait_send()
        for k in range(3):
            max_copy(j, k).wait_send()
    for k in range(3):
        r1(k).wait_send()
        r2(k).wait_send()
    for k in range(Z // 2):
        r3(k, 0).wait_send()
        if k < Z // 2 - 1:
            r3(k, 1).wait_send()
    r4.wait_send()
    for j in range(CHUNKS):
        for d in range(2):
            forward_copy(j, d).wait_recv()
            forward_copy(j, d).wait_send()


def write_kernel(out, sc, rout, ready_gate, ready_up, scale_gate, scale_up, router, sem, sc_sem, r_sem):
    copies = []
    for j in range(CHUNKS):
        cols = pl.ds((j % PER) * WIDTH, WIDTH)
        for x in range(X):
            copies.append(
                pltpu.make_async_copy(
                    out.at[j, x],
                    (ready_gate, ready_up)[j // PER].at[0, pl.ds(x * ROWS, ROWS), cols],
                    sem.at[j, x],
                )
            )
        copies.append(
            pltpu.make_async_copy(
                sc.at[j], (scale_gate, scale_up)[j // PER].at[:, cols], sc_sem.at[j]
            )
        )
    copies.append(pltpu.make_async_copy(rout, router, r_sem))
    for c in copies:
        c.start()
    for c in copies:
        c.wait()


def per_device(train_gate, other_gate, train_up, other_up, mix_share, router_weight, router_gain):
    f32, bf16 = jnp.float32, jnp.bfloat16
    hbm = pl.BlockSpec(memory_space=pltpu.HBM)
    vmem = pl.BlockSpec(memory_space=pltpu.VMEM)
    dma = pltpu.SemaphoreType.DMA
    out, sc, rout = pl.pallas_call(
        main_kernel,
        out_shape=(
            pltpu.VMEM((CHUNKS, X, ROWS, WIDTH), bf16),
            pltpu.VMEM((CHUNKS, 1, WIDTH), f32),
            pltpu.VMEM((2 * Y * Z, X * ROWS), bf16),
        ),
        in_specs=[pl.BlockSpec(memory_space=pltpu.SMEM)] + [hbm] * 6,
        out_specs=(vmem, vmem, vmem),
        scratch_shapes=[
            pltpu.VMEM((CHUNKS, ROWS, WIDTH), f32),
            pltpu.VMEM((CHUNKS, ROWS, WIDTH), f32),
            pltpu.VMEM((CHUNKS, X, 1, WIDTH), f32),
            pltpu.VMEM((1, ROWS), f32),
            pltpu.VMEM((1, ROWS), f32),
            pltpu.VMEM((2, Z, Y, X, 4, 128), f32),
            pltpu.VMEM((2 * Y * Z, X * ROWS), f32),
            dma((CHUNKS, 2)), dma((2,)),
            dma((CHUNKS, 3)), dma((CHUNKS, 3)),
            dma((CHUNKS, 2, 2)), dma((CHUNKS, 2, 2)),
            dma((CHUNKS, 2)), dma((CHUNKS, 2)),
            dma((3,)), dma((3,)), dma((3,)), dma((3,)),
            dma((Z // 2, 2)), dma((Z // 2, 2)),
            dma, dma,
        ],
        compiler_params=pltpu.CompilerParams(
            collective_id=0, has_side_effects=True, vmem_limit_bytes=40 * 1024 * 1024
        ),
        name="gather",
    )(
        mix_share,
        *(
            pltpu.with_memory_space_constraint(a, pltpu.HBM)
            for a in (
                train_gate, other_gate, train_up, other_up,
                router_weight.reshape(1, ROWS), router_gain.reshape(1, ROWS),
            )
        )
    )
    ready_gate, ready_up, scale_gate, scale_up, router = pl.pallas_call(
        write_kernel,
        out_shape=(
            jax.ShapeDtypeStruct((1, X * ROWS, COLS), bf16),
            jax.ShapeDtypeStruct((1, X * ROWS, COLS), bf16),
            jax.ShapeDtypeStruct((1, COLS), f32),
            jax.ShapeDtypeStruct((1, COLS), f32),
            jax.ShapeDtypeStruct((2 * Y * Z, X * ROWS), bf16),
        ),
        in_specs=[vmem] * 3,
        out_specs=(hbm,) * 5,
        scratch_shapes=[dma((CHUNKS, X)), dma((CHUNKS,)), dma],
        compiler_params=pltpu.CompilerParams(vmem_limit_bytes=1024 * 1024),
        name="write",
    )(*(pltpu.with_memory_space_constraint(a, pltpu.VMEM) for a in (out, sc, rout)))
    return ready_gate, ready_up, scale_gate, scale_up, router.T


def solution(mesh):
    placed = (
        P("ep", "fsdp", None),
        P("ep", "fsdp", None),
        P("ep", "fsdp", None),
        P("ep", "fsdp", None),
        P("ep"),
        P("fsdp", "ep"),
        P("fsdp"),
    )
    return jax.shard_map(
        per_device,
        mesh=mesh,
        in_specs=placed,
        out_specs=(P("ep", None, None), P("ep", None, None), P("ep", None), P("ep", None), P()),
        check_vma=False,
    )
```

time: 127 us -> 109 us (0.86)
  Pallas kernels: 0 us -> 108 us
  waiting for transfers between devices: 46.1 us -> 0 us
  blocking collectives: 46 us -> 0 us
  between operations: 14.8 us -> 1.29 us
  other arithmetic: 10.6 us -> 0 us
  local copies, waits for them, and re-layouts: 9.61 us -> 0 us
    pallas_call x0 -> x2, Pallas kernels: none -> 108 us  [the longest x1 104 us: per_device(): pl.pallas_call(main_kernel, out_shape=(pltpu.VMEM((CHUNKS, X, ROWS, WIDTH...]
    all_gather x1 -> x0, waiting for transfers between devices: 46.1 us -> none  [side_by_side(): out = lax.all_gather(both, axis, axis=dim, tiled=True)]
    all_to_all x2 -> x0, blocking collectives: 37.9 us -> none  [sent_to_all(): lax.all_to_all(jnp.broadcast_to(array[None], (length, *array.shape)), axi...]
    all_gather x1 -> x0, blocking collectives: 8.13 us -> none  [per_device(): row_router = lax.all_gather(part_router, 'fsdp', axis=0, tiled=True)]
    split x1 -> x0, local copies, waits for them, and re-layouts: 6.02 us -> none  [side_by_side(): jnp.split(out, [sum(widths[:k]) for k in range(1, len(widths))], axis=along)]
    convert_element_type x2 -> x0, other arithmetic: 3.96 us -> none  [the longest x1 3.95 us: per_device(): (latest_up / jnp.expand_dims(scale_up, 1)).astype(jnp.bfloat16)]
    reduce_max x3 -> x0, other arithmetic: 2.96 us -> none  [the longest x1 2.63 us: per_device(): jnp.max(jnp.abs(latest_gate), axis=1)]
    unnamed x16 -> x0, local copies, waits for them, and re-layouts: 2.71 us -> none
  transfers between devices with their start and end apart: 1 -> 0, of which waited for: 1 -> 0; matrix products, arithmetic and copies ran while one was open for 3% -> 0% of each run, Pallas kernels for 0% -> 0%
where the time goes in v1:
time: 109 us
  Pallas kernels  108 us (99%)
  between operations  1.29 us (1%)
    pallas_call x1, Pallas kernels, per_device(): pl.pallas_call(main_kernel, out_shape=(pltpu.VMEM((CHUNKS, X, ROWS, WIDTH...  104 us
    pallas_call x1, Pallas kernels, per_device(): pl.pallas_call(write_kernel, out_shape=(jax.ShapeDtypeStruct((1, X * ROWS...  3.73 us

profile of v1, /device:TPU:1, one launch (start us, length us, event | category | flops | bytes accessed | tf_op | source)
XLA Modules:
  0.0 109.4 jit_solution(5616684496829991952)
XLA Ops:
  1.3 104.4 %gather.1 = (bf16[8,4,512,256]{3,2,1,0:T(8,128)(2,1)S(1)}, f32[8,1,256]{2,1,0:T(1,128)S(1)}, bf16[64,2048]{1,0:T(8,128)(2,1)S(1)}) custom-call(f32[1]{0:T(128)S(6)} %copy.12.share, f32[1,512,1024]{2,1,0:T(8,128)} %tg.1, f32[1,512,1024]{2,1,0:T(8,128)} %og.1, f32[1,512,1024]{2,1,0:T(8,128)} %tu.1, f32[1,512,1024]{2,1,0:T(8,128)} %ou.1, f32[1,512]{1,0:T(1,128)} %bitcast.3, ...), custom_call_target="tpu_custom_call" | custom-call | tf_op jit(solution)/shard_map/gather/pallas_call | solution.py:249
  105.6 3.7 %write.1 = (bf16[1,2048,1024]{2,1,0:T(8,128)(2,1)}, bf16[1,2048,1024]{2,1,0:T(8,128)(2,1)}, f32[1,1024]{1,0:T(1,128)}, f32[1,1024]{1,0:T(1,128)}, bf16[64,2048]{1,0:T(8,128)(2,1)}) custom-call(bf16[8,4,512,256]{3,2,1,0:T(8,128)(2,1)S(1)} %get-tuple-element.13.out, f32[8,1,256]{2,1,0:T(1,128)S(1)} %get-tuple-element.14.sc, ...), custom_call_target="tpu_custom_call" | custom-call | tf_op jit(solution)/shard_map/write/pallas_call | solution.py:288

commit v2 on v1

--- a/solution.py
+++ b/solution.py
@@ -56,8 +56,9 @@
     for j in range(CHUNKS):
         load(j, 0).start()
         load(j, 1).start()
-    for c in small:
-        c.start()
+        if j == 0:
+            for c in small:
+                c.start()
 
     def max_copy(j, k):
         return pltpu.make_async_remote_copy(
@@ -83,6 +84,32 @@
             device_id=x_peers[d], device_id_type=MESH,
         )
 
+    def r1(k):
+        ref = rt.at[core, z, y, x]
+        return pltpu.make_async_remote_copy(
+            src_ref=ref, dst_ref=ref, send_sem=r1_send.at[k], recv_sem=r1_recv.at[k],
+            device_id=x_peers[k], device_id_type=MESH,
+        )
+
+    def r2(k):
+        ref = rt.at[core, z, y]
+        return pltpu.make_async_remote_copy(
+            src_ref=ref, dst_ref=ref, send_sem=r2_send.at[k], recv_sem=r2_recv.at[k],
+            device_id=y_peers[k], device_id_type=MESH,
+        )
+
+    def r3(k, d):
+        source = lax.rem(z + (Z - k if d == 0 else k), Z)
+        ref = rt.at[core, source]
+        return pltpu.make_async_remote_copy(
+            src_ref=ref, dst_ref=ref, send_sem=r3_send.at[k, d], recv_sem=r3_recv.at[k, d],
+            device_id=z_peers[d], device_id_type=MESH,
+        )
+
+    r4 = pltpu.make_async_remote_copy(
+        src_ref=rt.at[core], dst_ref=rt.at[core], send_sem=r4_send, recv_sem=r4_recv,
+        device_id=partner, device_id_type=MESH,
+    )
     share_t = share[0]
     share_o = 1.0 - share_t
 
@@ -102,6 +129,14 @@
             pl.semaphore_wait(barrier, 9)
         for k in (2, 0, 1):
             max_copy(j, k).start()
+        if j == 0:
+            for c in small:
+                c.wait()
+            piece = rwv[...] * rgv[...]
+            for r in range(4):
+                rt[core, z, y, x, pl.ds(r, 1), :] = piece[:, r * 128 : (r + 1) * 128]
+            for k in (2, 0, 1):
+                r1(k).start()
 
     for j in range(CHUNKS):
         for k in range(3):
@@ -121,40 +156,6 @@
             own_copy(j, 0, h).start()
             own_copy(j, 1, 1 - h).start()
 
-    for c in small:
-        c.wait()
-    piece = rwv[...] * rgv[...]
-    for r in range(4):
-        rt[core, z, y, x, pl.ds(r, 1), :] = piece[:, r * 128 : (r + 1) * 128]
-
-    def r1(k):
-        ref = rt.at[core, z, y, x]
-        return pltpu.make_async_remote_copy(
-            src_ref=ref, dst_ref=ref, send_sem=r1_send.at[k], recv_sem=r1_recv.at[k],
-            device_id=x_peers[k], device_id_type=MESH,
-        )
-
-    def r2(k):
-        ref = rt.at[core, z, y]
-        return pltpu.make_async_remote_copy(
-            src_ref=ref, dst_ref=ref, send_sem=r2_send.at[k], recv_sem=r2_recv.at[k],
-            device_id=y_peers[k], device_id_type=MESH,
-        )
-
-    def r3(k, d):
-        source = lax.rem(z + (Z - k if d == 0 else k), Z)
-        ref = rt.at[core, source]
-        return pltpu.make_async_remote_copy(
-            src_ref=ref, dst_ref=ref, send_sem=r3_send.at[k, d], recv_sem=r3_recv.at[k, d],
-            device_id=z_peers[d], device_id_type=MESH,
-        )
-
-    r4 = pltpu.make_async_remote_copy(
-        src_ref=rt.at[core], dst_ref=rt.at[core], send_sem=r4_send, recv_sem=r4_recv,
-        device_id=partner, device_id_type=MESH,
-    )
-    for k in range(3):
-        r1(k).start()
     for k in range(3):
         r1(k).wait_recv()
     for k in range(3):

time: 109 us -> 85.6 us (0.79); the launches traced: 109 us -> 84.6 us
  Pallas kernels: 108 us -> 83.3 us
    pallas_call x1, Pallas kernels: 104 us -> 79.6 us  [per_device(): pl.pallas_call(main_kernel, out_shape=(pltpu.VMEM((CHUNKS, X, ROWS, WIDTH...]
where the time goes in v2:
time: 85.6 us; the launch traced here: 84.6 us
  Pallas kernels  83.3 us (97%)
  between operations  1.29 us (2%)
    pallas_call x1, Pallas kernels, per_device(): pl.pallas_call(main_kernel, out_shape=(pltpu.VMEM((CHUNKS, X, ROWS, WIDTH...  79.6 us
    pallas_call x1, Pallas kernels, per_device(): pl.pallas_call(write_kernel, out_shape=(jax.ShapeDtypeStruct((1, X * ROWS...  3.73 us

profile of v2, /device:TPU:1, one launch (start us, length us, event | category | flops | bytes accessed | tf_op | source)
XLA Modules:
  0.0 84.6 jit_solution(5383776623344994689)
XLA Ops:
  1.3 79.6 %gather.1 = (bf16[8,4,512,256]{3,2,1,0:T(8,128)(2,1)S(1)}, f32[8,1,256]{2,1,0:T(1,128)S(1)}, bf16[64,2048]{1,0:T(8,128)(2,1)S(1)}) custom-call(f32[1]{0:T(128)S(6)} %copy.12.share, f32[1,512,1024]{2,1,0:T(8,128)} %tg.1, f32[1,512,1024]{2,1,0:T(8,128)} %og.1, f32[1,512,1024]{2,1,0:T(8,128)} %tu.1, f32[1,512,1024]{2,1,0:T(8,128)} %ou.1, f32[1,512]{1,0:T(1,128)} %bitcast.3, ...), custom_call_target="tpu_custom_call" | custom-call | tf_op jit(solution)/shard_map/gather/pallas_call | solution.py:250
  80.9 3.7 %write.1 = (bf16[1,2048,1024]{2,1,0:T(8,128)(2,1)}, bf16[1,2048,1024]{2,1,0:T(8,128)(2,1)}, f32[1,1024]{1,0:T(1,128)}, f32[1,1024]{1,0:T(1,128)}, bf16[64,2048]{1,0:T(8,128)(2,1)}) custom-call(bf16[8,4,512,256]{3,2,1,0:T(8,128)(2,1)S(1)} %get-tuple-element.13.out, f32[8,1,256]{2,1,0:T(1,128)S(1)} %get-tuple-element.14.sc, ...), custom_call_target="tpu_custom_call" | custom-call | tf_op jit(solution)/shard_map/write/pallas_call | solution.py:289

commit v3 on v2

--- a/solution.py
+++ b/solution.py
@@ -33,14 +33,21 @@
     right, left, opp = (lax.rem(x + k, X) for k in (1, X - 1, 2))
     x_peers = tuple({"fsdp": p} for p in (right, left, opp))
     at = lambda zz, yy, cc: {"ep": (zz * Y + yy) * 2 + cc}
-    y_peers = tuple(at(z, lax.rem(y + k, Y), core) for k in (1, 2, 3))
-    z_up, z_down = lax.rem(z + 1, Z), lax.rem(z + Z - 1, Z)
-    z_peers = (at(z_up, y, core), at(z_down, y, core))
+    y_up, y_down = at(z, lax.rem(y + 1, Y), core), at(z, lax.rem(y + Y - 1, Y), core)
+    z_up, z_down = at(lax.rem(z + 1, Z), y, core), at(lax.rem(z + Z - 1, Z), y, core)
     partner = at(z, y, 1 - core)
 
     barrier = pltpu.get_barrier_semaphore()
-    for peer in (*x_peers, *y_peers, *z_peers, partner):
+
+    def greet(peer):
         pl.semaphore_signal(barrier, inc=1, device_id=peer, device_id_type=MESH)
+
+    for peer in x_peers:
+        greet(peer)
+    pl.when(z < Z - 1)(lambda: greet(z_up))
+    pl.when(y < Y - 1)(lambda: greet(y_up))
+    pl.when(core == 0)(lambda: greet(partner))
+    greeted = 3 + jnp.minimum(z, 1) + jnp.minimum(y, 1) + core
 
     def load(j, which):
         src = ((tg, og), (tu, ou))[j // PER][which]
@@ -53,12 +60,9 @@
         pltpu.make_async_copy(rw, rwv, small_sem.at[0]),
         pltpu.make_async_copy(rg, rgv, small_sem.at[1]),
     )
-    for j in range(CHUNKS):
+    def start_loads(j):
         load(j, 0).start()
         load(j, 1).start()
-        if j == 0:
-            for c in small:
-                c.start()
 
     def max_copy(j, k):
         return pltpu.make_async_remote_copy(
@@ -91,20 +95,48 @@
             device_id=x_peers[k], device_id_type=MESH,
         )
 
-    def r2(k):
-        ref = rt.at[core, z, y]
-        return pltpu.make_async_remote_copy(
-            src_ref=ref, dst_ref=ref, send_sem=r2_send.at[k], recv_sem=r2_recv.at[k],
-            device_id=y_peers[k], device_id_type=MESH,
-        )
-
-    def r3(k, d):
-        source = lax.rem(z + (Z - k if d == 0 else k), Z)
-        ref = rt.at[core, source]
-        return pltpu.make_async_remote_copy(
-            src_ref=ref, dst_ref=ref, send_sem=r3_send.at[k, d], recv_sem=r3_recv.at[k, d],
-            device_id=z_peers[d], device_id_type=MESH,
-        )
+    def line_copy(ref, peer, send_sem, recv_sem):
+        return pltpu.make_async_remote_copy(
+            src_ref=ref, dst_ref=ref, send_sem=send_sem, recv_sem=recv_sem,
+            device_id=peer, device_id_type=MESH,
+        )
+
+    def along(pos, n, block, up_peer, down_peer, send, recv):
+        down = lambda k: line_copy(
+            block(lax.rem(pos + k, n)), down_peer, send.at[k, 0], recv.at[k, 0]
+        )
+        up = lambda k: line_copy(
+            block(lax.rem(pos + n - k, n)), up_peer, send.at[k, 1], recv.at[k, 1]
+        )
+        sends_down = lambda k: (pos >= 1) & (pos + k <= n - 1)
+        sends_up = lambda k: (pos <= n - 2) & (pos >= k)
+        gets_down = lambda k: pos + 1 + k <= n - 1
+        gets_up = lambda k: pos >= 1 + k
+
+        def run():
+            pl.when(sends_down(0))(lambda: down(0).start())
+            for k in range(n - 1):
+                pl.when(gets_down(k))(lambda: down(k).wait_recv())
+                if k + 1 < n - 1:
+                    pl.when(sends_down(k + 1))(lambda: down(k + 1).start())
+                if k > 0:
+                    pl.when(gets_up(k - 1))(lambda: up(k - 1).wait_recv())
+                pl.when(sends_up(k))(lambda: up(k).start())
+            pl.when(gets_up(n - 2))(lambda: up(n - 2).wait_recv())
+
+        def drain():
+            for k in range(n - 1):
+                pl.when(sends_down(k))(lambda: down(k).wait_send())
+                pl.when(sends_up(k))(lambda: up(k).wait_send())
+
+        return run, drain
+
+    run_y, drain_y = along(
+        y, Y, lambda i: rt.at[core, z, i], y_up, y_down, r2_send, r2_recv
+    )
+    run_z, drain_z = along(
+        z, Z, lambda i: rt.at[core, i], z_up, z_down, r3_send, r3_recv
+    )
 
     r4 = pltpu.make_async_remote_copy(
         src_ref=rt.at[core], dst_ref=rt.at[core], send_sem=r4_send, recv_sem=r4_recv,
@@ -113,7 +145,7 @@
     share_t = share[0]
     share_o = 1.0 - share_t
 
-    for j in range(CHUNKS):
+    def local(j):
         load(j, 0).wait()
         load(j, 1).wait()
 
@@ -125,8 +157,34 @@
 
         top = lax.fori_loop(0, ROWS // STEP, mix, jnp.zeros((8, WIDTH), jnp.float32), unroll=True)
         mx[j, x] = jnp.max(top, axis=0, keepdims=True)
+
+    def finish(j):
+        for k in range(3):
+            max_copy(j, k).wait_recv()
+        scale = jnp.maximum(
+            jnp.maximum(mx[j, 0], mx[j, 1]), jnp.maximum(mx[j, 2], mx[j, 3])
+        )
+        sc[j] = scale
+
+        def divide(i, carry):
+            rows = pl.ds(pl.multiple_of(i * STEP, STEP), STEP)
+            out[j, x, rows, :] = (tbuf[j, rows, :] / scale).astype(jnp.bfloat16)
+            return carry
+
+        for h in range(2):
+            lax.fori_loop(h * (HALF // STEP), (h + 1) * (HALF // STEP), divide, 0, unroll=True)
+            own_copy(j, 0, h).start()
+            own_copy(j, 1, h).start()
+
+    start_loads(0)
+    for c in small:
+        c.start()
+    for j in range(1, CHUNKS):
+        start_loads(j)
+    for j in range(CHUNKS):
+        local(j)
         if j == 0:
-            pl.semaphore_wait(barrier, 9)
+            pl.semaphore_wait(barrier, greeted)
         for k in (2, 0, 1):
             max_copy(j, k).start()
         if j == 0:
@@ -137,40 +195,24 @@
                 rt[core, z, y, x, pl.ds(r, 1), :] = piece[:, r * 128 : (r + 1) * 128]
             for k in (2, 0, 1):
                 r1(k).start()
-
-    for j in range(CHUNKS):
-        for k in range(3):
-            max_copy(j, k).wait_recv()
-        scale = jnp.maximum(
-            jnp.maximum(mx[j, 0], mx[j, 1]), jnp.maximum(mx[j, 2], mx[j, 3])
-        )
-        sc[j] = scale
-
-        def divide(i, carry):
-            rows = pl.ds(pl.multiple_of(i * STEP, STEP), STEP)
-            out[j, x, rows, :] = (tbuf[j, rows, :] / scale).astype(jnp.bfloat16)
-            return carry
-
-        lax.fori_loop(0, ROWS // STEP, divide, 0, unroll=True)
-        for h in range(2):
-            own_copy(j, 0, h).start()
-            own_copy(j, 1, 1 - h).start()
+        if j == 3:
+            finish(0)
+    for j in range(1, CHUNKS):
+        finish(j)
 
     for k in range(3):
         r1(k).wait_recv()
-    for k in range(3):
-        r2(k).start()
-    for k in range(3):
-        r2(k).wait_recv()
-    for k in range(Z // 2):
-        r3(k, 0).start()
-        if k < Z // 2 - 1:
-            r3(k, 1).start()
-        r3(k, 0).wait_recv()
-        if k < Z // 2 - 1:
-            r3(k, 1).wait_recv()
-    r4.start()
+    run_y()
+    run_z()
+    for j in range(CHUNKS):
+        own_copy(j, 0, 0).wait_recv()
+        forward_copy(j, 0).start()
+        own_copy(j, 1, 1).wait_recv()
+        forward_copy(j, 1).start()
+
+    pl.when(core == 1)(lambda: r4.start())
     r4.wait_recv()
+    pl.when(core == 0)(lambda: r4.start())
 
     def spread(zz, carry):
         rows = pl.ds(pl.multiple_of(zz * 2 * Y, 2 * Y), 2 * Y)
@@ -189,12 +231,6 @@
         return carry
 
     lax.fori_loop(0, 4, narrow, 0)
-
-    for j in range(CHUNKS):
-        own_copy(j, 0, 0).wait_recv()
-        forward_copy(j, 0).start()
-        own_copy(j, 1, 1).wait_recv()
-        forward_copy(j, 1).start()
 
     for j in range(CHUNKS):
         own_copy(j, 0, 1).wait_recv()
@@ -206,11 +242,8 @@
             max_copy(j, k).wait_send()
     for k in range(3):
         r1(k).wait_send()
-        r2(k).wait_send()
-    for k in range(Z // 2):
-        r3(k, 0).wait_send()
-        if k < Z // 2 - 1:
-            r3(k, 1).wait_send()
+    drain_y()
+    drain_z()
     r4.wait_send()
     for j in range(CHUNKS):
         for d in range(2):
@@ -268,8 +301,8 @@
             dma((CHUNKS, 3)), dma((CHUNKS, 3)),
             dma((CHUNKS, 2, 2)), dma((CHUNKS, 2, 2)),
             dma((CHUNKS, 2)), dma((CHUNKS, 2)),
-            dma((3,)), dma((3,)), dma((3,)), dma((3,)),
-            dma((Z // 2, 2)), dma((Z // 2, 2)),
+            dma((3,)), dma((3,)), dma((Y - 1, 2)), dma((Y - 1, 2)),
+            dma((Z - 1, 2)), dma((Z - 1, 2)),
             dma, dma,
         ],
         compiler_params=pltpu.CompilerParams(

time: 85.6 us -> 82.3 us (0.961)
  Pallas kernels: 83.3 us -> 80 us
    pallas_call x1, Pallas kernels: 79.6 us -> 76.3 us  [per_device(): pl.pallas_call(main_kernel, out_shape=(pltpu.VMEM((CHUNKS, X, ROWS, WIDTH...]
where the time goes in v3:
time: 82.3 us; the launch traced here: 81.3 us
  Pallas kernels  80 us (97%)
  between operations  1.29 us (2%)
    pallas_call x1, Pallas kernels, per_device(): pl.pallas_call(main_kernel, out_shape=(pltpu.VMEM((CHUNKS, X, ROWS, WIDTH...  76.3 us
    pallas_call x1, Pallas kernels, per_device(): pl.pallas_call(write_kernel, out_shape=(jax.ShapeDtypeStruct((1, X * ROWS...  3.73 us

profile of v3, /device:TPU:1, one launch (start us, length us, event | category | flops | bytes accessed | tf_op | source)
XLA Modules:
  0.0 81.3 jit_solution(17782627122734082284)
XLA Ops:
  1.3 76.3 %gather.1 = (bf16[8,4,512,256]{3,2,1,0:T(8,128)(2,1)S(1)}, f32[8,1,256]{2,1,0:T(1,128)S(1)}, bf16[64,2048]{1,0:T(8,128)(2,1)S(1)}) custom-call(f32[1]{0:T(128)S(6)} %copy.12.share, f32[1,512,1024]{2,1,0:T(8,128)} %tg.1, f32[1,512,1024]{2,1,0:T(8,128)} %og.1, f32[1,512,1024]{2,1,0:T(8,128)} %tu.1, f32[1,512,1024]{2,1,0:T(8,128)} %ou.1, f32[1,512]{1,0:T(1,128)} %bitcast.3, ...), custom_call_target="tpu_custom_call" | custom-call | tf_op jit(solution)/shard_map/gather/pallas_call | solution.py:283
  77.5 3.7 %write.1 = (bf16[1,2048,1024]{2,1,0:T(8,128)(2,1)}, bf16[1,2048,1024]{2,1,0:T(8,128)(2,1)}, f32[1,1024]{1,0:T(1,128)}, f32[1,1024]{1,0:T(1,128)}, bf16[64,2048]{1,0:T(8,128)(2,1)}) custom-call(bf16[8,4,512,256]{3,2,1,0:T(8,128)(2,1)S(1)} %get-tuple-element.13.out, f32[8,1,256]{2,1,0:T(1,128)S(1)} %get-tuple-element.14.sc, ...), custom_call_target="tpu_custom_call" | custom-call | tf_op jit(solution)/shard_map/write/pallas_call | solution.py:322

commit v4 on v3

--- a/solution.py
+++ b/solution.py
@@ -13,7 +13,8 @@
 WIDTH = 256
 PER = COLS // WIDTH
 CHUNKS = 2 * PER
-HALF = ROWS // 2
+OWN = (((0, 1), (1, 3), (4, 4)), ((0, 1), (4, 4), (1, 3)))
+ONWARD = (((0, 4), (0, 1)), ((4, 4), (1,)))
 STEP = 64
 
 
@@ -71,20 +72,23 @@
             device_id=x_peers[k], device_id_type=MESH,
         )
 
-    def own_copy(j, d, h):
-        piece = out.at[j, x, pl.ds(h * HALF, HALF)]
+    def block(chunks, device):
+        first, number = chunks
+        return out.at[pl.ds(first, number), pl.ds(pl.multiple_of(device * ROWS, ROWS), ROWS)]
+
+    def own_copy(d, i):
+        piece = block(OWN[d][i], x)
         return pltpu.make_async_remote_copy(
             src_ref=piece, dst_ref=piece,
-            send_sem=own_send.at[j, d, h], recv_sem=own_recv.at[j, d, h],
+            send_sem=own_send.at[d, i], recv_sem=own_recv.at[d, i],
             device_id=x_peers[d], device_id_type=MESH,
         )
 
-    def forward_copy(j, d):
-        source = (left, right)[d]
-        piece = out.at[j, source, pl.ds(d * HALF, HALF)]
+    def forward_copy(d):
+        piece = block(ONWARD[d][0], (left, right)[d])
         return pltpu.make_async_remote_copy(
             src_ref=piece, dst_ref=piece,
-            send_sem=fwd_send.at[j, d], recv_sem=fwd_recv.at[j, d],
+            send_sem=fwd_send.at[d], recv_sem=fwd_recv.at[d],
             device_id=x_peers[d], device_id_type=MESH,
         )
 
@@ -113,7 +117,7 @@
         gets_down = lambda k: pos + 1 + k <= n - 1
         gets_up = lambda k: pos >= 1 + k
 
-        def run():
+        def run(between=lambda k: None):
             pl.when(sends_down(0))(lambda: down(0).start())
             for k in range(n - 1):
                 pl.when(gets_down(k))(lambda: down(k).wait_recv())
@@ -122,6 +126,7 @@
                 if k > 0:
                     pl.when(gets_up(k - 1))(lambda: up(k - 1).wait_recv())
                 pl.when(sends_up(k))(lambda: up(k).start())
+                between(k)
             pl.when(gets_up(n - 2))(lambda: up(n - 2).wait_recv())
 
         def drain():
@@ -164,17 +169,15 @@
         scale = jnp.maximum(
             jnp.maximum(mx[j, 0], mx[j, 1]), jnp.maximum(mx[j, 2], mx[j, 3])
         )
-        sc[j] = scale
+        sc[j // PER, :, (j % PER) * WIDTH : (j % PER + 1) * WIDTH] = scale
 
         def divide(i, carry):
             rows = pl.ds(pl.multiple_of(i * STEP, STEP), STEP)
-            out[j, x, rows, :] = (tbuf[j, rows, :] / scale).astype(jnp.bfloat16)
+            own_rows = pl.ds(pl.multiple_of(x * ROWS + i * STEP, STEP), STEP)
+            out[j, own_rows, :] = (tbuf[j, rows, :] / scale).astype(jnp.bfloat16)
             return carry
 
-        for h in range(2):
-            lax.fori_loop(h * (HALF // STEP), (h + 1) * (HALF // STEP), divide, 0, unroll=True)
-            own_copy(j, 0, h).start()
-            own_copy(j, 1, h).start()
+        lax.fori_loop(0, ROWS // STEP, divide, 0, unroll=True)
 
     start_loads(0)
     for c in small:
@@ -195,21 +198,24 @@
                 rt[core, z, y, x, pl.ds(r, 1), :] = piece[:, r * 128 : (r + 1) * 128]
             for k in (2, 0, 1):
                 r1(k).start()
-        if j == 3:
-            finish(0)
-    for j in range(1, CHUNKS):
+    sent = [0, 0]
+    for j in range(CHUNKS):
         finish(j)
+        for d in range(2):
+            while sent[d] < len(OWN[d]) and sum(OWN[d][sent[d]]) <= j + 1:
+                own_copy(d, sent[d]).start()
+                sent[d] += 1
 
     for k in range(3):
         r1(k).wait_recv()
+    def forward(d):
+        for i in ONWARD[d][1]:
+            own_copy(d, i).wait_recv()
+        forward_copy(d).start()
+
     run_y()
-    run_z()
-    for j in range(CHUNKS):
-        own_copy(j, 0, 0).wait_recv()
-        forward_copy(j, 0).start()
-        own_copy(j, 1, 1).wait_recv()
-        forward_copy(j, 1).start()
-
+    run_z(lambda k: forward(0) if k == 3 else None)
+    forward(1)
     pl.when(core == 1)(lambda: r4.start())
     r4.wait_recv()
     pl.when(core == 0)(lambda: r4.start())
@@ -232,12 +238,12 @@
 
     lax.fori_loop(0, 4, narrow, 0)
 
+    for d in range(2):
+        for i in range(len(OWN[d])):
+            if i not in ONWARD[d][1]:
+                own_copy(d, i).wait_recv()
+            own_copy(d, i).wait_send()
     for j in range(CHUNKS):
-        own_copy(j, 0, 1).wait_recv()
-        own_copy(j, 1, 0).wait_recv()
-        for d in range(2):
-            for h in range(2):
-                own_copy(j, d, h).wait_send()
         for k in range(3):
             max_copy(j, k).wait_send()
     for k in range(3):
@@ -245,29 +251,22 @@
     drain_y()
     drain_z()
     r4.wait_send()
-    for j in range(CHUNKS):
-        for d in range(2):
-            forward_copy(j, d).wait_recv()
-            forward_copy(j, d).wait_send()
+    for d in range(2):
+        forward_copy(d).wait_recv()
+        forward_copy(d).wait_send()
 
 
 def write_kernel(out, sc, rout, ready_gate, ready_up, scale_gate, scale_up, router, sem, sc_sem, r_sem):
     copies = []
     for j in range(CHUNKS):
         cols = pl.ds((j % PER) * WIDTH, WIDTH)
-        for x in range(X):
-            copies.append(
-                pltpu.make_async_copy(
-                    out.at[j, x],
-                    (ready_gate, ready_up)[j // PER].at[0, pl.ds(x * ROWS, ROWS), cols],
-                    sem.at[j, x],
-                )
-            )
         copies.append(
             pltpu.make_async_copy(
-                sc.at[j], (scale_gate, scale_up)[j // PER].at[:, cols], sc_sem.at[j]
+                out.at[j], (ready_gate, ready_up)[j // PER].at[0, :, cols], sem.at[j]
             )
         )
+    for m, scale in enumerate((scale_gate, scale_up)):
+        copies.append(pltpu.make_async_copy(sc.at[m], scale, sc_sem.at[m]))
     copies.append(pltpu.make_async_copy(rout, router, r_sem))
     for c in copies:
         c.start()
@@ -283,8 +282,8 @@
     out, sc, rout = pl.pallas_call(
         main_kernel,
         out_shape=(
-            pltpu.VMEM((CHUNKS, X, ROWS, WIDTH), bf16),
-            pltpu.VMEM((CHUNKS, 1, WIDTH), f32),
+            pltpu.VMEM((CHUNKS, X * ROWS, WIDTH), bf16),
+            pltpu.VMEM((2, 1, COLS), f32),
             pltpu.VMEM((2 * Y * Z, X * ROWS), bf16),
         ),
         in_specs=[pl.BlockSpec(memory_space=pltpu.SMEM)] + [hbm] * 6,
@@ -299,8 +298,7 @@
             pltpu.VMEM((2 * Y * Z, X * ROWS), f32),
             dma((CHUNKS, 2)), dma((2,)),
             dma((CHUNKS, 3)), dma((CHUNKS, 3)),
-            dma((CHUNKS, 2, 2)), dma((CHUNKS, 2, 2)),
-            dma((CHUNKS, 2)), dma((CHUNKS, 2)),
+            dma((2, 3)), dma((2, 3)), dma((2,)), dma((2,)),
             dma((3,)), dma((3,)), dma((Y - 1, 2)), dma((Y - 1, 2)),
             dma((Z - 1, 2)), dma((Z - 1, 2)),
             dma, dma,
@@ -330,7 +328,7 @@
         ),
         in_specs=[vmem] * 3,
         out_specs=(hbm,) * 5,
-        scratch_shapes=[dma((CHUNKS, X)), dma((CHUNKS,)), dma],
+        scratch_shapes=[dma((CHUNKS,)), dma((2,)), dma],
         compiler_params=pltpu.CompilerParams(vmem_limit_bytes=1024 * 1024),
         name="write",
     )(*(pltpu.with_memory_space_constraint(a, pltpu.VMEM) for a in (out, sc, rout)))

time: 82.3 us -> 81.2 us (0.987)
  Pallas kernels: 80 us -> 79.1 us
where the time goes in v4:
time: 81.2 us; the launch traced here: 80.4 us
  Pallas kernels  79.1 us (97%)
  between operations  1.29 us (2%)
    pallas_call x1, Pallas kernels, per_device(): pl.pallas_call(main_kernel, out_shape=(pltpu.VMEM((CHUNKS, X * ROWS, WIDT...  75.6 us
    pallas_call x1, Pallas kernels, per_device(): pl.pallas_call(write_kernel, out_shape=(jax.ShapeDtypeStruct((1, X * ROWS...  3.45 us

profile of v4, /device:TPU:1, one launch (start us, length us, event | category | flops | bytes accessed | tf_op | source)
XLA Modules:
  0.0 80.4 jit_solution(11161353295338118983)
XLA Ops:
  1.3 75.6 %gather.1 = (bf16[8,2048,256]{2,1,0:T(8,128)(2,1)S(1)}, f32[2,1,1024]{2,1,0:T(1,128)S(1)}, bf16[64,2048]{1,0:T(8,128)(2,1)S(1)}) custom-call(f32[1]{0:T(128)S(6)} %copy.12.share, f32[1,512,1024]{2,1,0:T(8,128)} %tg.1, f32[1,512,1024]{2,1,0:T(8,128)} %og.1, f32[1,512,1024]{2,1,0:T(8,128)} %tu.1, f32[1,512,1024]{2,1,0:T(8,128)} %ou.1, f32[1,512]{1,0:T(1,128)} %bitcast.3, ...), custom_call_target="tpu_custom_call" | custom-call | tf_op jit(solution)/shard_map/gather/pallas_call | solution.py:282
  76.9 3.5 %write.1 = (bf16[1,2048,1024]{2,1,0:T(8,128)(2,1)}, bf16[1,2048,1024]{2,1,0:T(8,128)(2,1)}, f32[1,1024]{1,0:T(1,128)}, f32[1,1024]{1,0:T(1,128)}, bf16[64,2048]{1,0:T(8,128)(2,1)}) custom-call(bf16[8,2048,256]{2,1,0:T(8,128)(2,1)S(1)} %get-tuple-element.13.out, f32[2,1,1024]{2,1,0:T(1,128)S(1)} %get-tuple-element.14.sc, ...), custom_call_target="tpu_custom_call" | custom-call | tf_op jit(solution)/shard_map/write/pallas_call | solution.py:320

commit v5 on v4

--- a/solution.py
+++ b/solution.py
@@ -16,13 +16,14 @@
 OWN = (((0, 1), (1, 3), (4, 4)), ((0, 1), (4, 4), (1, 3)))
 ONWARD = (((0, 4), (0, 1)), ((4, 4), (1,)))
 STEP = 64
+EARLY = 128
 
 
 def main_kernel(
     share, tg, og, tu, ou, rw, rg,
     out, sc, rout,
-    tbuf, obuf, mx, rwv, rgv, rt, stage,
-    ld_sem, small_sem, mx_send, mx_recv, own_send, own_recv, fwd_send, fwd_recv,
+    tbuf, obuf, early, mx, rwv, rgv, rt, stage,
+    ld_sem, small_sem, early_send, early_recv, mx_send, mx_recv, own_send, own_recv, fwd_send, fwd_recv,
     r1_send, r1_recv, r2_send, r2_recv, r3_send, r3_recv, r4_send, r4_recv,
 ):
     x = lax.axis_index("fsdp")
@@ -72,12 +73,13 @@
             device_id=x_peers[k], device_id_type=MESH,
         )
 
-    def block(chunks, device):
+    def block(chunks, device, skip=0):
         first, number = chunks
-        return out.at[pl.ds(first, number), pl.ds(pl.multiple_of(device * ROWS, ROWS), ROWS)]
+        rows = pl.ds(pl.multiple_of(device * ROWS + skip, STEP), ROWS - skip)
+        return out.at[pl.ds(first, number), rows]
 
     def own_copy(d, i):
-        piece = block(OWN[d][i], x)
+        piece = block(OWN[d][i], x, EARLY if i == 0 else 0)
         return pltpu.make_async_remote_copy(
             src_ref=piece, dst_ref=piece,
             send_sem=own_send.at[d, i], recv_sem=own_recv.at[d, i],
@@ -89,6 +91,13 @@
         return pltpu.make_async_remote_copy(
             src_ref=piece, dst_ref=piece,
             send_sem=fwd_send.at[d], recv_sem=fwd_recv.at[d],
+            device_id=x_peers[d], device_id_type=MESH,
+        )
+
+    def early_copy(d):
+        return pltpu.make_async_remote_copy(
+            src_ref=tbuf.at[0, pl.ds(0, EARLY)], dst_ref=early.at[d],
+            send_sem=early_send.at[d], recv_sem=early_recv.at[d],
             device_id=x_peers[d], device_id_type=MESH,
         )
 
@@ -163,6 +172,15 @@
         top = lax.fori_loop(0, ROWS // STEP, mix, jnp.zeros((8, WIDTH), jnp.float32), unroll=True)
         mx[j, x] = jnp.max(top, axis=0, keepdims=True)
 
+    def divide(j, device, scale, source, number):
+        def step(i, carry):
+            rows = pl.ds(pl.multiple_of(i * STEP, STEP), STEP)
+            put = pl.ds(pl.multiple_of(device * ROWS + i * STEP, STEP), STEP)
+            out[j, put, :] = (source[rows, :] / scale).astype(jnp.bfloat16)
+            return carry
+
+        lax.fori_loop(0, number // STEP, step, 0, unroll=True)
+
     def finish(j):
         for k in range(3):
             max_copy(j, k).wait_recv()
@@ -171,17 +189,11 @@
         )
         sc[j // PER, :, (j % PER) * WIDTH : (j % PER + 1) * WIDTH] = scale
 
-        def divide(i, carry):
-            rows = pl.ds(pl.multiple_of(i * STEP, STEP), STEP)
-            own_rows = pl.ds(pl.multiple_of(x * ROWS + i * STEP, STEP), STEP)
-            out[j, own_rows, :] = (tbuf[j, rows, :] / scale).astype(jnp.bfloat16)
-            return carry
-
-        lax.fori_loop(0, ROWS // STEP, divide, 0, unroll=True)
-
-    start_loads(0)
+        divide(j, x, scale, tbuf.at[j], ROWS)
+
     for c in small:
         c.start()
+    start_loads(0)
     for j in range(1, CHUNKS):
         start_loads(j)
     for j in range(CHUNKS):
@@ -191,13 +203,17 @@
         for k in (2, 0, 1):
             max_copy(j, k).start()
         if j == 0:
-            for c in small:
-                c.wait()
-            piece = rwv[...] * rgv[...]
-            for r in range(4):
-                rt[core, z, y, x, pl.ds(r, 1), :] = piece[:, r * 128 : (r + 1) * 128]
-            for k in (2, 0, 1):
-                r1(k).start()
+            for d in range(2):
+                early_copy(d).start()
+
+    for c in small:
+        c.wait()
+    piece = rwv[...] * rgv[...]
+    for r in range(4):
+        rt[core, z, y, x, pl.ds(r, 1), :] = piece[:, r * 128 : (r + 1) * 128]
+    for k in (2, 0, 1):
+        r1(k).start()
+
     sent = [0, 0]
     for j in range(CHUNKS):
         finish(j)
@@ -205,6 +221,10 @@
             while sent[d] < len(OWN[d]) and sum(OWN[d][sent[d]]) <= j + 1:
                 own_copy(d, sent[d]).start()
                 sent[d] += 1
+
+    for d, source in enumerate((left, right)):
+        early_copy(d).wait_recv()
+        divide(0, source, sc[0, :, :WIDTH], early.at[d], EARLY)
 
     for k in range(3):
         r1(k).wait_recv()
@@ -248,6 +268,8 @@
             max_copy(j, k).wait_send()
     for k in range(3):
         r1(k).wait_send()
+    for d in range(2):
+        early_copy(d).wait_send()
     drain_y()
     drain_z()
     r4.wait_send()
@@ -291,12 +313,13 @@
         scratch_shapes=[
             pltpu.VMEM((CHUNKS, ROWS, WIDTH), f32),
             pltpu.VMEM((CHUNKS, ROWS, WIDTH), f32),
+            pltpu.VMEM((2, EARLY, WIDTH), f32),
             pltpu.VMEM((CHUNKS, X, 1, WIDTH), f32),
             pltpu.VMEM((1, ROWS), f32),
             pltpu.VMEM((1, ROWS), f32),
             pltpu.VMEM((2, Z, Y, X, 4, 128), f32),
             pltpu.VMEM((2 * Y * Z, X * ROWS), f32),
-            dma((CHUNKS, 2)), dma((2,)),
+            dma((CHUNKS, 2)), dma((2,)), dma((2,)), dma((2,)),
             dma((CHUNKS, 3)), dma((CHUNKS, 3)),
             dma((2, 3)), dma((2, 3)), dma((2,)), dma((2,)),
             dma((3,)), dma((3,)), dma((Y - 1, 2)), dma((Y - 1, 2)),

time: 81.2 us -> 80.3 us (0.989)
  no operation moved by 1% of the time
where the time goes in v5:
time: 80.3 us; the launch traced here: 80.2 us
  Pallas kernels  78.9 us (98%)
  between operations  1.29 us (2%)
    pallas_call x1, Pallas kernels, per_device(): pl.pallas_call(main_kernel, out_shape=(pltpu.VMEM((CHUNKS, X * ROWS, WIDT...  75.4 us
    pallas_call x1, Pallas kernels, per_device(): pl.pallas_call(write_kernel, out_shape=(jax.ShapeDtypeStruct((1, X * ROWS...  3.45 us

profile of v5, /device:TPU:1, one launch (start us, length us, event | category | flops | bytes accessed | tf_op | source)
XLA Modules:
  0.0 80.2 jit_solution(13851584247208967864)
XLA Ops:
  1.3 75.4 %gather.1 = (bf16[8,2048,256]{2,1,0:T(8,128)(2,1)S(1)}, f32[2,1,1024]{2,1,0:T(1,128)S(1)}, bf16[64,2048]{1,0:T(8,128)(2,1)S(1)}) custom-call(f32[1]{0:T(128)S(6)} %copy.12.share, f32[1,512,1024]{2,1,0:T(8,128)} %tg.1, f32[1,512,1024]{2,1,0:T(8,128)} %og.1, f32[1,512,1024]{2,1,0:T(8,128)} %tu.1, f32[1,512,1024]{2,1,0:T(8,128)} %ou.1, f32[1,512]{1,0:T(1,128)} %bitcast.3, ...), custom_call_target="tpu_custom_call" | custom-call | tf_op jit(solution)/shard_map/gather/pallas_call | solution.py:304
  76.7 3.5 %write.1 = (bf16[1,2048,1024]{2,1,0:T(8,128)(2,1)}, bf16[1,2048,1024]{2,1,0:T(8,128)(2,1)}, f32[1,1024]{1,0:T(1,128)}, f32[1,1024]{1,0:T(1,128)}, bf16[64,2048]{1,0:T(8,128)(2,1)}) custom-call(bf16[8,2048,256]{2,1,0:T(8,128)(2,1)S(1)} %get-tuple-element.13.out, f32[2,1,1024]{2,1,0:T(1,128)S(1)} %get-tuple-element.14.sc, ...), custom_call_target="tpu_custom_call" | custom-call | tf_op jit(solution)/shard_map/write/pallas_call | solution.py:343

commit v6 on v5

--- a/solution.py
+++ b/solution.py
@@ -13,6 +13,7 @@
 WIDTH = 256
 PER = COLS // WIDTH
 CHUNKS = 2 * PER
+GROUPS = ((0, 1), (1, 3), (4, 4))
 OWN = (((0, 1), (1, 3), (4, 4)), ((0, 1), (4, 4), (1, 3)))
 ONWARD = (((0, 4), (0, 1)), ((4, 4), (1,)))
 STEP = 64
@@ -22,8 +23,9 @@
 def main_kernel(
     share, tg, og, tu, ou, rw, rg,
     out, sc, rout,
-    tbuf, obuf, early, mx, rwv, rgv, rt, stage,
-    ld_sem, small_sem, early_send, early_recv, mx_send, mx_recv, own_send, own_recv, fwd_send, fwd_recv,
+    buf, early, mx, rgw, rt, stage,
+    ld_sem, small_sem, early_send, early_recv, mx_send, mx_recv,
+    own_send, own_recv, fwd_send, fwd_recv,
     r1_send, r1_recv, r2_send, r2_recv, r3_send, r3_recv, r4_send, r4_recv,
 ):
     x = lax.axis_index("fsdp")
@@ -51,25 +53,35 @@
     pl.when(core == 0)(lambda: greet(partner))
     greeted = 3 + jnp.minimum(z, 1) + jnp.minimum(y, 1) + core
 
-    def load(j, which):
-        src = ((tg, og), (tu, ou))[j // PER][which]
-        cols = pl.ds((j % PER) * WIDTH, WIDTH)
-        return pltpu.make_async_copy(
-            src.at[0, :, cols], (tbuf, obuf)[which].at[j], ld_sem.at[j, which]
-        )
-
     small = (
-        pltpu.make_async_copy(rw, rwv, small_sem.at[0]),
-        pltpu.make_async_copy(rg, rgv, small_sem.at[1]),
-    )
-    def start_loads(j):
-        load(j, 0).start()
-        load(j, 1).start()
-
-    def max_copy(j, k):
-        return pltpu.make_async_remote_copy(
-            src_ref=mx.at[j, x], dst_ref=mx.at[j, x],
-            send_sem=mx_send.at[j, k], recv_sem=mx_recv.at[j, k],
+        pltpu.make_async_copy(rw, rgw.at[0], small_sem),
+        pltpu.make_async_copy(rg, rgw.at[1], small_sem),
+    )
+
+    def start_loads(g):
+        first, number = GROUPS[g]
+        for j in range(first, first + number):
+            cols = pl.ds((j % PER) * WIDTH, WIDTH)
+            for which, src in enumerate(((tg, og), (tu, ou))[j // PER]):
+                pltpu.make_async_copy(src.at[0, :, cols], buf.at[which, j], ld_sem.at[g]).start()
+
+    def wait_loads(g):
+        all_of_it = buf.at[:, pl.ds(*GROUPS[g])]
+        pltpu.make_async_copy(all_of_it, all_of_it, ld_sem.at[g]).wait()
+
+    def as_many(ref, sem):
+        return pltpu.make_async_remote_copy(
+            src_ref=ref, dst_ref=ref, send_sem=sem, recv_sem=sem,
+            device_id=x_peers[0], device_id_type=MESH,
+        )
+
+    def out_rows(number, rows):
+        return out.at[pl.ds(0, number), pl.ds(0, rows)]
+
+    def max_copy(g, k):
+        mine = mx.at[pl.ds(*GROUPS[g]), x]
+        return pltpu.make_async_remote_copy(
+            src_ref=mine, dst_ref=mine, send_sem=mx_send, recv_sem=mx_recv.at[g],
             device_id=x_peers[k], device_id_type=MESH,
         )
 
@@ -82,7 +94,7 @@
         piece = block(OWN[d][i], x, EARLY if i == 0 else 0)
         return pltpu.make_async_remote_copy(
             src_ref=piece, dst_ref=piece,
-            send_sem=own_send.at[d, i], recv_sem=own_recv.at[d, i],
+            send_sem=own_send, recv_sem=own_recv.at[d, 0 if i in ONWARD[d][1] else 1],
             device_id=x_peers[d], device_id_type=MESH,
         )
 
@@ -90,21 +102,21 @@
         piece = block(ONWARD[d][0], (left, right)[d])
         return pltpu.make_async_remote_copy(
             src_ref=piece, dst_ref=piece,
-            send_sem=fwd_send.at[d], recv_sem=fwd_recv.at[d],
+            send_sem=fwd_send, recv_sem=fwd_recv,
             device_id=x_peers[d], device_id_type=MESH,
         )
 
     def early_copy(d):
         return pltpu.make_async_remote_copy(
-            src_ref=tbuf.at[0, pl.ds(0, EARLY)], dst_ref=early.at[d],
-            send_sem=early_send.at[d], recv_sem=early_recv.at[d],
+            src_ref=buf.at[0, 0, pl.ds(0, EARLY)], dst_ref=early.at[d],
+            send_sem=early_send, recv_sem=early_recv,
             device_id=x_peers[d], device_id_type=MESH,
         )
 
     def r1(k):
         ref = rt.at[core, z, y, x]
         return pltpu.make_async_remote_copy(
-            src_ref=ref, dst_ref=ref, send_sem=r1_send.at[k], recv_sem=r1_recv.at[k],
+            src_ref=ref, dst_ref=ref, send_sem=r1_send, recv_sem=r1_recv,
             device_id=x_peers[k], device_id_type=MESH,
         )
 
@@ -116,32 +128,41 @@
 
     def along(pos, n, block, up_peer, down_peer, send, recv):
         down = lambda k: line_copy(
-            block(lax.rem(pos + k, n)), down_peer, send.at[k, 0], recv.at[k, 0]
+            block(lax.rem(pos + k, n)), down_peer, send.at[0], recv.at[k, 0]
         )
         up = lambda k: line_copy(
-            block(lax.rem(pos + n - k, n)), up_peer, send.at[k, 1], recv.at[k, 1]
+            block(lax.rem(pos + n - k, n)), up_peer, send.at[1], recv.at[k, 1]
         )
         sends_down = lambda k: (pos >= 1) & (pos + k <= n - 1)
         sends_up = lambda k: (pos <= n - 2) & (pos >= k)
         gets_down = lambda k: pos + 1 + k <= n - 1
         gets_up = lambda k: pos >= 1 + k
 
+        def next_down(k):
+            if k > 0:
+                down(k - 1).wait_send()
+            down(k).start()
+
+        def next_up(k):
+            if k > 0:
+                up(k - 1).wait_send()
+            up(k).start()
+
         def run(between=lambda k: None):
-            pl.when(sends_down(0))(lambda: down(0).start())
+            pl.when(sends_down(0))(lambda: next_down(0))
             for k in range(n - 1):
                 pl.when(gets_down(k))(lambda: down(k).wait_recv())
                 if k + 1 < n - 1:
-                    pl.when(sends_down(k + 1))(lambda: down(k + 1).start())
+                    pl.when(sends_down(k + 1))(lambda: next_down(k + 1))
                 if k > 0:
                     pl.when(gets_up(k - 1))(lambda: up(k - 1).wait_recv())
-                pl.when(sends_up(k))(lambda: up(k).start())
+                pl.when(sends_up(k))(lambda: next_up(k))
                 between(k)
             pl.when(gets_up(n - 2))(lambda: up(n - 2).wait_recv())
 
         def drain():
-            for k in range(n - 1):
-                pl.when(sends_down(k))(lambda: down(k).wait_send())
-                pl.when(sends_up(k))(lambda: up(k).wait_send())
+            pl.when(sends_down(0))(lambda: down(0).wait_send())
+            pl.when(sends_up(0))(lambda: up(0).wait_send())
 
         return run, drain
 
@@ -160,13 +181,10 @@
     share_o = 1.0 - share_t
 
     def local(j):
-        load(j, 0).wait()
-        load(j, 1).wait()
-
         def mix(i, top):
             rows = pl.ds(pl.multiple_of(i * STEP, STEP), STEP)
-            latest = share_t * tbuf[j, rows, :] + share_o * obuf[j, rows, :]
-            tbuf[j, rows, :] = latest
+            latest = share_t * buf[0, j, rows, :] + share_o * buf[1, j, rows, :]
+            buf[0, j, rows, :] = latest
             return jnp.maximum(top, jnp.max(jnp.abs(latest).reshape(STEP // 8, 8, WIDTH), axis=0))
 
         top = lax.fori_loop(0, ROWS // STEP, mix, jnp.zeros((8, WIDTH), jnp.float32), unroll=True)
@@ -182,33 +200,31 @@
         lax.fori_loop(0, number // STEP, step, 0, unroll=True)
 
     def finish(j):
-        for k in range(3):
-            max_copy(j, k).wait_recv()
         scale = jnp.maximum(
             jnp.maximum(mx[j, 0], mx[j, 1]), jnp.maximum(mx[j, 2], mx[j, 3])
         )
         sc[j // PER, :, (j % PER) * WIDTH : (j % PER + 1) * WIDTH] = scale
 
-        divide(j, x, scale, tbuf.at[j], ROWS)
+        divide(j, x, scale, buf.at[0, j], ROWS)
 
     for c in small:
         c.start()
-    start_loads(0)
-    for j in range(1, CHUNKS):
-        start_loads(j)
-    for j in range(CHUNKS):
-        local(j)
-        if j == 0:
+    for g in range(len(GROUPS)):
+        start_loads(g)
+    for g, (first, number) in enumerate(GROUPS):
+        wait_loads(g)
+        for j in range(first, first + number):
+            local(j)
+        if g == 0:
             pl.semaphore_wait(barrier, greeted)
         for k in (2, 0, 1):
-            max_copy(j, k).start()
-        if j == 0:
+            max_copy(g, k).start()
+        if g == 0:
             for d in range(2):
                 early_copy(d).start()
 
-    for c in small:
-        c.wait()
-    piece = rwv[...] * rgv[...]
+    pltpu.make_async_copy(rgw, rgw, small_sem).wait()
+    piece = rgw[0] * rgw[1]
     for r in range(4):
         rt[core, z, y, x, pl.ds(r, 1), :] = piece[:, r * 128 : (r + 1) * 128]
     for k in (2, 0, 1):
@@ -216,21 +232,28 @@
 
     sent = [0, 0]
     for j in range(CHUNKS):
+        for g, (first, number) in enumerate(GROUPS):
+            if j == first:
+                as_many(mx.at[pl.ds(first, number), pl.ds(0, X - 1)], mx_recv.at[g]).wait_recv()
         finish(j)
         for d in range(2):
             while sent[d] < len(OWN[d]) and sum(OWN[d][sent[d]]) <= j + 1:
                 own_copy(d, sent[d]).start()
                 sent[d] += 1
 
+    as_many(early, early_recv).wait_recv()
     for d, source in enumerate((left, right)):
-        early_copy(d).wait_recv()
         divide(0, source, sc[0, :, :WIDTH], early.at[d], EARLY)
 
-    for k in range(3):
-        r1(k).wait_recv()
+    r1_all = as_many(rt.at[core, z, y, pl.ds(0, X - 1)], r1_recv)
+    r1_all.wait_recv()
+    own_rows = CHUNKS * ROWS - EARLY
+    onward_rows = [
+        sum(OWN[d][i][1] * ROWS - (EARLY if i == 0 else 0) for i in ONWARD[d][1]) for d in range(2)
+    ]
+
     def forward(d):
-        for i in ONWARD[d][1]:
-            own_copy(d, i).wait_recv()
+        as_many(out_rows(1, onward_rows[d]), own_recv.at[d, 0]).wait_recv()
         forward_copy(d).start()
 
     run_y()
@@ -259,41 +282,30 @@
     lax.fori_loop(0, 4, narrow, 0)
 
     for d in range(2):
-        for i in range(len(OWN[d])):
-            if i not in ONWARD[d][1]:
-                own_copy(d, i).wait_recv()
-            own_copy(d, i).wait_send()
-    for j in range(CHUNKS):
-        for k in range(3):
-            max_copy(j, k).wait_send()
-    for k in range(3):
-        r1(k).wait_send()
-    for d in range(2):
-        early_copy(d).wait_send()
+        as_many(out_rows(1, own_rows - onward_rows[d]), own_recv.at[d, 1]).wait_recv()
+    as_many(out_rows(4, own_rows // 2), own_send).wait_send()
+    as_many(mx.at[:, pl.ds(0, X - 1)], mx_send).wait_send()
+    as_many(rt.at[core, z, y, pl.ds(0, X - 1)], r1_send).wait_send()
+    as_many(early, early_send).wait_send()
     drain_y()
     drain_z()
     r4.wait_send()
-    for d in range(2):
-        forward_copy(d).wait_recv()
-        forward_copy(d).wait_send()
+    as_many(out_rows(2, X * ROWS), fwd_recv).wait_recv()
+    as_many(out_rows(2, X * ROWS), fwd_send).wait_send()
 
 
 def write_kernel(out, sc, rout, ready_gate, ready_up, scale_gate, scale_up, router, sem, sc_sem, r_sem):
-    copies = []
     for j in range(CHUNKS):
         cols = pl.ds((j % PER) * WIDTH, WIDTH)
-        copies.append(
-            pltpu.make_async_copy(
-                out.at[j], (ready_gate, ready_up)[j // PER].at[0, :, cols], sem.at[j]
-            )
-        )
+        ready = (ready_gate, ready_up)[j // PER]
+        pltpu.make_async_copy(out.at[j], ready.at[0, :, cols], sem).start()
     for m, scale in enumerate((scale_gate, scale_up)):
-        copies.append(pltpu.make_async_copy(sc.at[m], scale, sc_sem.at[m]))
-    copies.append(pltpu.make_async_copy(rout, router, r_sem))
-    for c in copies:
-        c.start()
-    for c in copies:
-        c.wait()
+        pltpu.make_async_copy(sc.at[m], scale, sc_sem).start()
+    routed = pltpu.make_async_copy(rout, router, r_sem)
+    routed.start()
+    pltpu.make_async_copy(sc, sc, sc_sem).wait()
+    routed.wait()
+    pltpu.make_async_copy(out, out, sem).wait()
 
 
 def per_device(train_gate, other_gate, train_up, other_up, mix_share, router_weight, router_gain):
@@ -311,20 +323,15 @@
         in_specs=[pl.BlockSpec(memory_space=pltpu.SMEM)] + [hbm] * 6,
         out_specs=(vmem, vmem, vmem),
         scratch_shapes=[
-            pltpu.VMEM((CHUNKS, ROWS, WIDTH), f32),
-            pltpu.VMEM((CHUNKS, ROWS, WIDTH), f32),
+            pltpu.VMEM((2, CHUNKS, ROWS, WIDTH), f32),
             pltpu.VMEM((2, EARLY, WIDTH), f32),
             pltpu.VMEM((CHUNKS, X, 1, WIDTH), f32),
-            pltpu.VMEM((1, ROWS), f32),
-            pltpu.VMEM((1, ROWS), f32),
+            pltpu.VMEM((2, 1, ROWS), f32),
             pltpu.VMEM((2, Z, Y, X, 4, 128), f32),
             pltpu.VMEM((2 * Y * Z, X * ROWS), f32),
-            dma((CHUNKS, 2)), dma((2,)), dma((2,)), dma((2,)),
-            dma((CHUNKS, 3)), dma((CHUNKS, 3)),
-            dma((2, 3)), dma((2, 3)), dma((2,)), dma((2,)),
-            dma((3,)), dma((3,)), dma((Y - 1, 2)), dma((Y - 1, 2)),
-            dma((Z - 1, 2)), dma((Z - 1, 2)),
-            dma, dma,
+            dma((len(GROUPS),)), dma, dma, dma, dma, dma((len(GROUPS),)),
+            dma, dma((2, 2)), dma, dma,
+            dma, dma, dma((2,)), dma((Y - 1, 2)), dma((2,)), dma((Z - 1, 2)), dma, dma,
         ],
         compiler_params=pltpu.CompilerParams(
             collective_id=0, has_side_effects=True, vmem_limit_bytes=40 * 1024 * 1024
@@ -351,7 +358,7 @@
         ),
         in_specs=[vmem] * 3,
         out_specs=(hbm,) * 5,
-        scratch_shapes=[dma((CHUNKS,)), dma((2,)), dma],
+        scratch_shapes=[dma, dma, dma],
         compiler_params=pltpu.CompilerParams(vmem_limit_bytes=1024 * 1024),
         name="write",
     )(*(pltpu.with_memory_space_constraint(a, pltpu.VMEM) for a in (out, sc, rout)))

time: 80.3 us -> 79.4 us (0.989)
  Pallas kernels: 78.9 us -> 78 us
where the time goes in v6:
time: 79.4 us; the launch traced here: 79.3 us
  Pallas kernels  78 us (98%)
  between operations  1.29 us (2%)
    pallas_call x1, Pallas kernels, per_device(): pl.pallas_call(main_kernel, out_shape=(pltpu.VMEM((CHUNKS, X * ROWS, WIDT...  74.6 us
    pallas_call x1, Pallas kernels, per_device(): pl.pallas_call(write_kernel, out_shape=(jax.ShapeDtypeStruct((1, X * ROWS...  3.38 us

profile of v6, /device:TPU:1, one launch (start us, length us, event | category | flops | bytes accessed | tf_op | source)
XLA Modules:
  0.0 79.3 jit_solution(7131739101284440537)
XLA Ops:
  1.3 74.6 %gather.1 = (bf16[8,2048,256]{2,1,0:T(8,128)(2,1)S(1)}, f32[2,1,1024]{2,1,0:T(1,128)S(1)}, bf16[64,2048]{1,0:T(8,128)(2,1)S(1)}) custom-call(f32[1]{0:T(128)S(6)} %copy.12.share, f32[1,512,1024]{2,1,0:T(8,128)} %tg.1, f32[1,512,1024]{2,1,0:T(8,128)} %og.1, f32[1,512,1024]{2,1,0:T(8,128)} %tu.1, f32[1,512,1024]{2,1,0:T(8,128)} %ou.1, f32[1,512]{1,0:T(1,128)} %bitcast.3, ...), custom_call_target="tpu_custom_call" | custom-call | tf_op jit(solution)/shard_map/gather/pallas_call | solution.py:316
  75.9 3.4 %write.1 = (bf16[1,2048,1024]{2,1,0:T(8,128)(2,1)}, bf16[1,2048,1024]{2,1,0:T(8,128)(2,1)}, f32[1,1024]{1,0:T(1,128)}, f32[1,1024]{1,0:T(1,128)}, bf16[64,2048]{1,0:T(8,128)(2,1)}) custom-call(bf16[8,2048,256]{2,1,0:T(8,128)(2,1)S(1)} %get-tuple-element.13.out, f32[2,1,1024]{2,1,0:T(1,128)S(1)} %get-tuple-element.14.sc, ...), custom_call_target="tpu_custom_call" | custom-call | tf_op jit(solution)/shard_map/write/pallas_call | solution.py:350

commit v7 on v6

--- a/solution.py
+++ b/solution.py
@@ -16,8 +16,8 @@
 GROUPS = ((0, 1), (1, 3), (4, 4))
 OWN = (((0, 1), (1, 3), (4, 4)), ((0, 1), (4, 4), (1, 3)))
 ONWARD = (((0, 4), (0, 1)), ((4, 4), (1,)))
-STEP = 64
-EARLY = 128
+STEP = 16
+EARLY = 112
 
 
 def main_kernel(
@@ -46,12 +46,8 @@
     def greet(peer):
         pl.semaphore_signal(barrier, inc=1, device_id=peer, device_id_type=MESH)
 
-    for peer in x_peers:
+    for peer in (x_peers[2], x_peers[0], x_peers[1]):
         greet(peer)
-    pl.when(z < Z - 1)(lambda: greet(z_up))
-    pl.when(y < Y - 1)(lambda: greet(y_up))
-    pl.when(core == 0)(lambda: greet(partner))
-    greeted = 3 + jnp.minimum(z, 1) + jnp.minimum(y, 1) + core
 
     small = (
         pltpu.make_async_copy(rw, rgw.at[0], small_sem),
@@ -207,9 +203,14 @@
 
         divide(j, x, scale, buf.at[0, j], ROWS)
 
+    start_loads(0)
+    pl.when(z < Z - 1)(lambda: greet(z_up))
+    pl.when(y < Y - 1)(lambda: greet(y_up))
+    pl.when(core == 0)(lambda: greet(partner))
+    greeted = 3 + jnp.minimum(z, 1) + jnp.minimum(y, 1) + core
     for c in small:
         c.start()
-    for g in range(len(GROUPS)):
+    for g in range(1, len(GROUPS)):
         start_loads(g)
     for g, (first, number) in enumerate(GROUPS):
         wait_loads(g)

time: 79.4 us -> 79.2 us (level)
  no operation moved by 1% of the time
where the time goes in v7:
time: 79.2 us; the launch traced here: 79 us
  Pallas kernels  77.8 us (98%)
  between operations  1.29 us (2%)
    pallas_call x1, Pallas kernels, per_device(): pl.pallas_call(main_kernel, out_shape=(pltpu.VMEM((CHUNKS, X * ROWS, WIDT...  74.4 us
    pallas_call x1, Pallas kernels, per_device(): pl.pallas_call(write_kernel, out_shape=(jax.ShapeDtypeStruct((1, X * ROWS...  3.38 us

profile of v7, /device:TPU:1, one launch (start us, length us, event | category | flops | bytes accessed | tf_op | source)
XLA Modules:
  0.0 79.0 jit_solution(16185665949223612861)
XLA Ops:
  1.3 74.4 %gather.1 = (bf16[8,2048,256]{2,1,0:T(8,128)(2,1)S(1)}, f32[2,1,1024]{2,1,0:T(1,128)S(1)}, bf16[64,2048]{1,0:T(8,128)(2,1)S(1)}) custom-call(f32[1]{0:T(128)S(6)} %copy.12.share, f32[1,512,1024]{2,1,0:T(8,128)} %tg.1, f32[1,512,1024]{2,1,0:T(8,128)} %og.1, f32[1,512,1024]{2,1,0:T(8,128)} %tu.1, f32[1,512,1024]{2,1,0:T(8,128)} %ou.1, f32[1,512]{1,0:T(1,128)} %bitcast.3, ...), custom_call_target="tpu_custom_call" | custom-call | tf_op jit(solution)/shard_map/gather/pallas_call | solution.py:317
  75.7 3.4 %write.1 = (bf16[1,2048,1024]{2,1,0:T(8,128)(2,1)}, bf16[1,2048,1024]{2,1,0:T(8,128)(2,1)}, f32[1,1024]{1,0:T(1,128)}, f32[1,1024]{1,0:T(1,128)}, bf16[64,2048]{1,0:T(8,128)(2,1)}) custom-call(bf16[8,2048,256]{2,1,0:T(8,128)(2,1)S(1)} %get-tuple-element.13.out, f32[2,1,1024]{2,1,0:T(1,128)S(1)} %get-tuple-element.14.sc, ...), custom_call_target="tpu_custom_call" | custom-call | tf_op jit(solution)/shard_map/write/pallas_call | solution.py:351
